TPU v7x, 32 devices: a whole 2x2x4 slice. The times are simulated.
32 devices in a mesh: owner: 4 (over y, core), rows: 8 (over z, x).
Axes of the slice: x: 2, y: 2, z: 4, core: 2. Of those that a mesh axis runs over, the one named last changes fastest.
Arguments:
- w_down: float32 [16, 6400, 4096], P('owner', None, 'rows'), may hold values from -0.109375 to 0.109375
- avg_down: bfloat16 [16, 6400, 4096], P('owner', None, 'rows'), may hold values from -0.0390625 to 0.0390625
- router_weight: float32 [4096, 16], P('rows', 'owner'), may hold values from -0.09375 to 0.09375
- router_gain: float32 [4096], P('rows'), may hold values from 0.25 to 1.75
Outputs:
- serve_down: bfloat16 [16, 6400, 4096], P('owner', 'rows')
- scale_down: float32 [16, 6400], P('owner', 'rows')
- serve_router: bfloat16 [4096, 16], replicated
All inputs are finite; a program needn't handle non-finite values.
Results may differ from a plain program's by a relative error of at most 0.0085.
Values may be sent and summed in bfloat16 or wider, within the bound.
A program may use at most 256 MiB of HBM per device.

v0:
```python
import jax
import jax.numpy as jnp
from jax import lax
from jax.sharding import PartitionSpec as P


def local(w_down, avg_down, router_weight, router_gain):
    fresh_down = w_down + avg_down.astype(jnp.float32)
    total_down = lax.psum(
        jnp.sum(fresh_down * fresh_down, axis=2).astype(jnp.bfloat16), "rows"
    ).astype(jnp.float32)
    scale_down = jnp.sqrt(total_down)
    narrow_down = (fresh_down / jnp.expand_dims(scale_down, 2)).astype(jnp.bfloat16)
    serve_down = lax.all_to_all(narrow_down, "rows", split_axis=1, concat_axis=2, tiled=True)
    scale_down = lax.dynamic_slice_in_dim(
        scale_down, lax.axis_index("rows") * serve_down.shape[1], serve_down.shape[1], axis=1
    )
    part_router = (router_weight * router_gain[:, None]).astype(jnp.bfloat16)
    row_router = lax.all_gather(part_router, "rows", axis=0, tiled=True)
    serve_router = lax.all_gather(row_router, "owner", axis=1, tiled=True)
    return (serve_down, scale_down, serve_router)


def solution(mesh):
    return jax.shard_map(
        local,
        mesh=mesh,
        in_specs=(
            P("owner", None, "rows"),
            P("owner", None, "rows"),
            P("rows", "owner"),
            P("rows"),
        ),
        out_specs=(P("owner", "rows", None), P("owner", "rows"), P()),
        check_vma=False,
    )
```

profile of v0, /device:TPU:0, one launch (start us, length us, event | category | flops | bytes accessed | tf_op | source)
XLA Modules:
  0.0 826.9 jit_solution(7862156734528137198)
XLA Ops:
  0.6 24.2 %multiply_reduce_fusion = bf16[4,6400]{1,0:T(4,128)(2,1)S(1)} fusion(f32[4,6400,512]{2,1,0:T(8,128)} %param.4, bf16[4,6400,512]{2,1,0:T(8,128)(2,1)} %param.5), kind=kLoop, calls=%fused_computation.1 | loop fusion | flops 52403200 | bytes 78694400 | tf_op jit(solution)/shard_map/reduce_sum | solution.py:10
  24.9 0.9 copy.21
  25.8 83.5 %psum.7 = bf16[4,6400]{0,1:T(8,128)(2,1)} all-reduce(bf16[4,6400]{0,1:T(8,128)(2,1)S(1)} %copy.21), channel_id=1, replica_groups=mesh['owner'=4,'rows'=8] {'rows'}, use_global_device_ids=true, to_apply=%region_1.0 | all-reduce | flops 25600 | bytes 102400 | tf_op jit(solution)/shard_map/psum | solution.py:9
  109.3 2.3 convert_sqrt_fusion
  111.6 1.2 copy.17
  112.8 34.3 %divide_convert_fusion = bf16[4,6400,512]{2,1,0:T(8,128)(2,1)} fusion(f32[4,6400,512]{2,1,0:T(8,128)} %param.4, bf16[4,6400,512]{2,1,0:T(8,128)(2,1)} %param.5, f32[4,6400]{1,0:T(4,128)S(1)} %copy.17), kind=kLoop, calls=%fused_computation | loop fusion | flops 52428800 | bytes 104960000 | tf_op jit(solution)/shard_map/convert_element_type | solution.py:13
  147.1 33.4 %copy.18 = bf16[4,6400,512]{2,0,1:T(4,128)(2,1)} copy(bf16[4,6400,512]{2,1,0:T(8,128)(2,1)} %divide_convert_fusion) | data formatting | bytes 52428800 | tf_op jit(solution)/shard_map/convert_element_type | solution.py:13
  180.5 0.0 copy-start
  180.5 0.0 copy-start.1
  180.5 6.6 all-to-all-start
  187.2 0.8 constant_dynamic-slice_fusion
  187.9 1.8 copy.20
  189.7 0.0 copy-done
  189.7 0.0 copy-done.1
  189.7 573.7 %all_gather.6 = bf16[4096,4]{0,1:T(4,128)(2,1)S(1)} all-gather(bf16[512,4]{0,1:T(4,128)(2,1)S(1)} %multiply_convert_fusion), channel_id=1, replica_groups=mesh['owner'=4,'rows'=8] {'rows'}, dimensions={0}, use_global_device_ids=true | all-gather | bytes 36864 | tf_op jit(solution)/shard_map/all_gather | solution.py:19
  763.4 5.4 all-gather
  768.8 0.7 reshape.9
  769.5 0.0 all-to-all-done
  769.5 18.2 %copy.19 = bf16[4,800,8,512]{3,2,1,0:T(8,128)(2,1)} copy(bf16[4,800,8,512]{3,0,1,2:T(4,128)(2,1)} %bitcast.1) | data formatting | bytes 52428800 | tf_op jit(solution)/shard_map/all_to_all | solution.py:14
  787.7 39.2 %all_to_all.16 = bf16[4,800,4096]{2,1,0:T(8,128)(2,1)} reshape(bf16[4,800,8,512]{3,2,1,0:T(8,128)(2,1)} %copy.19) | data formatting | bytes 52428800 | tf_op jit(solution)/shard_map/all_to_all | solution.py:14
  (1 shorter events, 0.0 us)
Async XLA Ops:
  180.5 9.2 %copy-start = (f32[512,4]{0,1:T(4,128)S(1)}, f32[512,4]{0,1:T(4,128)}, u32[]{:S(2)}) copy-start(f32[512,4]{0,1:T(4,128)} %param.6) | copy-start | bytes 24580
  180.5 9.2 %copy-start.1 = (f32[512]{0:T(512)S(1)}, f32[512]{0:T(512)}, u32[]{:S(2)}) copy-start(f32[512]{0:T(512)} %param.7) | copy-start | bytes 6148
  180.5 589.0 %all-to-all-start = ((bf16[4,6400,512]{2,0,1:T(4,128)(2,1)}), bf16[4,6400,512]{2,0,1:T(4,128)(2,1)}, u32[]{:S(2)}, u32[]{:S(2)}) async-start(bf16[4,6400,512]{2,0,1:T(4,128)(2,1)} %copy.18), calls=%async_computation | async-start | bytes 52428800 | tf_op jit(solution)/shard_map/all_to_all | solution.py:14
where the time goes:
time: 828 us; the launch traced here: 827 us
  blocking collectives  663 us (80%)
  local copies, waits for them, and re-layouts  96.2 us (12%)
  other arithmetic  60.8 us (7%)
    all_gather x1, blocking collectives, local(): row_router = lax.all_gather(part_router, 'rows', axis=0, tiled=True)  574 us
    psum x1, blocking collectives, local(): lax.psum(jnp.sum(fresh_down * fresh_down, axis=2).astype(jnp.bfloat16), '...  83.5 us
    all_to_all x2, local copies, waits for them, and re-layouts, local(): lax.all_to_all(narrow_down, 'rows', split_axis=1, concat_axis=2, tiled=True)  57.4 us
    convert_element_type x1, other arithmetic, local(): (fresh_down / jnp.expand_dims(scale_down, 2)).astype(jnp.bfloat16)  34.3 us
    convert_element_type x1, local copies, waits for them, and re-layouts, local(): (fresh_down / jnp.expand_dims(scale_down, 2)).astype(jnp.bfloat16)  33.4 us
    reduce_sum x1, other arithmetic, local(): jnp.sum(fresh_down * fresh_down, axis=2).astype(jnp.bfloat16)  24.2 us
  transfers between devices with their start and end apart: 1, of which 0 were waited for; matrix products, arithmetic and copies ran while one was open for 0% of the time, Pallas kernels for 0%

commit v1 on v0

--- a/solution.py
+++ b/solution.py
@@ -11,7 +11,12 @@
     ).astype(jnp.float32)
     scale_down = jnp.sqrt(total_down)
     narrow_down = (fresh_down / jnp.expand_dims(scale_down, 2)).astype(jnp.bfloat16)
-    serve_down = lax.all_to_all(narrow_down, "rows", split_axis=1, concat_axis=2, tiled=True)
+    serve_down = jnp.concatenate(
+        lax.all_to_all(
+            jnp.stack(jnp.split(narrow_down, lax.axis_size("rows"), axis=1)), "rows", 0, 0
+        ),
+        axis=2,
+    )
     scale_down = lax.dynamic_slice_in_dim(
         scale_down, lax.axis_index("rows") * serve_down.shape[1], serve_down.shape[1], axis=1
     )

time: 828 us -> 739 us (0.89)
  local copies, waits for them, and re-layouts: 96.2 us -> 49.8 us
  blocking collectives: 663 us -> 623 us
    all_to_all x2 -> x0, local copies, waits for them, and re-layouts: 57.4 us -> none  [local(): lax.all_to_all(narrow_down, 'rows', split_axis=1, concat_axis=2, tiled=True)]
    psum x1, blocking collectives: 83.5 us -> 39.3 us  [local(): lax.psum(jnp.sum(fresh_down * fresh_down, axis=2).astype(jnp.bfloat16), '...]
    convert_element_type x1 -> x0, local copies, waits for them, and re-layouts: 33.4 us -> none  [local(): (fresh_down / jnp.expand_dims(scale_down, 2)).astype(jnp.bfloat16)]
    unnamed x7 -> x12, local copies, waits for them, and re-layouts: 3.4 us -> 27.5 us
    reshape x0 -> x1, local copies, waits for them, and re-layouts: none -> 17.9 us  [local(): jnp.concatenate(lax.all_to_all(jnp.stack(jnp.split(narrow_down, lax.axis_...]
where the time goes in v1:
time: 739 us
  blocking collectives  623 us (84%)
  other arithmetic  58.6 us (8%)
  local copies, waits for them, and re-layouts  49.8 us (7%)
    all_gather x1, blocking collectives, local(): row_router = lax.all_gather(part_router, 'rows', axis=0, tiled=True)  578 us
    psum x1, blocking collectives, local(): lax.psum(jnp.sum(fresh_down * fresh_down, axis=2).astype(jnp.bfloat16), '...  39.3 us
    convert_element_type x1, other arithmetic, local(): (fresh_down / jnp.expand_dims(scale_down, 2)).astype(jnp.bfloat16)  34.3 us
    unnamed x12, local copies, waits for them, and re-layouts  27.5 us
    reduce_sum x1, other arithmetic, local(): jnp.sum(fresh_down * fresh_down, axis=2).astype(jnp.bfloat16)  24.2 us
    reshape x1, local copies, waits for them, and re-layouts, local(): jnp.concatenate(lax.all_to_all(jnp.stack(jnp.split(narrow_down, lax.axis_...  17.9 us
  transfers between devices with their start and end apart: 1, of which 0 were waited for; matrix products, arithmetic and copies ran while one was open for 0% of the time, Pallas kernels for 0%

profile of v1, /device:TPU:0, one launch (start us, length us, event | category | flops | bytes accessed | tf_op | source)
XLA Modules:
  0.0 738.6 jit_solution(8709787585122454427)
XLA Ops:
  0.6 24.2 %multiply_reduce_fusion = bf16[4,6400]{1,0:T(4,128)(2,1)S(1)} fusion(f32[4,6400,512]{2,1,0:T(8,128)} %param.4, bf16[4,6400,512]{2,1,0:T(8,128)(2,1)} %param.5), kind=kLoop, calls=%fused_computation.1 | loop fusion | flops 52403200 | bytes 78694400 | tf_op jit(solution)/shard_map/reduce_sum | solution.py:10
  24.9 39.3 %psum.7 = bf16[4,6400]{1,0:T(4,128)(2,1)S(1)} all-reduce(bf16[4,6400]{1,0:T(4,128)(2,1)S(1)} %multiply_reduce_fusion), channel_id=1, replica_groups=mesh['owner'=4,'rows'=8] {'rows'}, use_global_device_ids=true, to_apply=%region_1.0 | all-reduce | flops 25600 | bytes 102400 | tf_op jit(solution)/shard_map/psum | solution.py:9
  64.2 0.1 convert_sqrt_fusion
  64.3 34.3 %divide_convert_fusion = bf16[4,6400,512]{2,1,0:T(8,128)(2,1)} fusion(f32[4,6400,512]{2,1,0:T(8,128)} %param.4, bf16[4,6400,512]{2,1,0:T(8,128)(2,1)} %param.5, f32[4,6400]{1,0:T(4,128)S(1)} %convert_sqrt_fusion), kind=kLoop, calls=%fused_computation | loop fusion | flops 52428800 | bytes 104960000 | tf_op jit(solution)/shard_map/convert_element_type | solution.py:13
  98.5 3.8 fusion.7
  102.4 3.8 fusion.6
  106.2 3.8 fusion.5
  110.0 3.8 fusion.4
  113.8 3.9 fusion.3
  117.7 3.8 fusion.2
  121.5 3.8 fusion.1
  125.3 3.8 fusion
  129.1 0.0 copy-start
  129.1 0.0 copy-start.1
  129.1 6.6 all-to-all-start
  135.8 0.0 copy-done
  135.8 0.0 copy-done.1
  135.8 578.1 %all_gather.6 = bf16[4096,4]{0,1:T(4,128)(2,1)S(1)} all-gather(bf16[512,4]{0,1:T(4,128)(2,1)S(1)} %multiply_convert_fusion), channel_id=1, replica_groups=mesh['owner'=4,'rows'=8] {'rows'}, dimensions={0}, use_global_device_ids=true | all-gather | bytes 36864 | tf_op jit(solution)/shard_map/all_gather | solution.py:24
  714.0 5.4 all-gather
  719.4 0.7 reshape.17
  720.1 0.7 constant_dynamic-slice_fusion
  720.7 0.0 all-to-all-done
  720.7 17.9 %copy.9 = bf16[8,4,100,8,512]{4,3,0,2,1:T(8,128)(2,1)} copy(bf16[8,4,100,8,512]{4,3,2,1,0:T(8,128)(2,1)} %bitcast.13) | data formatting | bytes 52428800 | tf_op jit(solution)/shard_map/reshape | solution.py:14
  (1 shorter events, 0.0 us)
Async XLA Ops:
  129.1 6.6 copy-start
  129.1 6.7 copy-start.1
  129.1 591.6 %all-to-all-start = ((bf16[8,4,800,512]{3,2,1,0:T(8,128)(2,1)}), bf16[8,4,800,512]{3,2,1,0:T(8,128)(2,1)}, u32[]{:S(2)}, u32[]{:S(2)}) async-start(bf16[8,4,800,512]{3,2,1,0:T(8,128)(2,1)} %fusion), calls=%async_computation | async-start | bytes 52428800 | tf_op jit(solution)/shard_map/all_to_all | solution.py:15
